TPU v7x, 256 devices: a whole 4x4x8 slice. The times are simulated.
256 devices in a mesh: seq: 32 (over y, z), tp: 8 (over x, core).
Axes of the slice: x: 4, y: 4, z: 8, core: 2. Of those that a mesh axis runs over, the one named last changes fastest.
Arguments:
- tokens: bfloat16 [24576, 2048], P('seq', 'tp'), may hold values from -20 to 20
- w_query: bfloat16 [2048, 2048], P(None, 'tp'), may hold values from -0.125 to 0.125
- w_key: bfloat16 [2048, 2048], P(None, 'tp'), may hold values from -0.125 to 0.125
- w_value: bfloat16 [2048, 2048], P(None, 'tp'), may hold values from -0.125 to 0.125
- head_gain: float32 [2048], P('tp'), may hold values from 0.5 to 1.5
- w_out: bfloat16 [2048, 2048], P('tp'), may hold values from -0.125 to 0.125
- norm_gain: float32 [2048], replicated, may hold values from 0.5 to 1.5
- w_gate: bfloat16 [2048, 8192], P('seq', 'tp'), may hold values from -0.125 to 0.125
- w_up: bfloat16 [2048, 8192], P('seq', 'tp'), may hold values from -0.125 to 0.125
- w_down: bfloat16 [8192, 2048], P('tp', 'seq'), may hold values from -0.0625 to 0.0625
Outputs:
- layer_out: bfloat16 [24576, 2048], P('seq', 'tp')
All inputs are finite; a program needn't handle non-finite values.
Results may differ from a plain program's by a relative error of at most 0.009.
Values may be sent and summed in bfloat16 or wider, within the bound.
No kernel may reach another device: no remote copies, remote signals or barrier semaphores. Data moves between devices by JAX's collectives and lax.ppermute only.
A program may use at most 128 MiB of HBM per device.

v0:
```python
import jax
import jax.numpy as jnp
from jax import lax
from jax.sharding import Mesh
from jax.sharding import PartitionSpec as P

HD = 128
SEQ = ("seq_0", "seq_1")


def nothing_yet(array, identity):
    return jnp.zeros_like(array) + jnp.asarray(identity, array.dtype)


def entering(array, axes, combine, identity):
    before = start = nothing_yet(array, identity)
    total = array
    for axis in reversed(axes):
        peers, position = (lax.axis_size(axis), lax.axis_index(axis))
        pieces = lax.all_gather(total.astype(jnp.bfloat16), axis)
        inside, total = (start, start)
        for k in range(peers):
            passed = k < position
            total = combine(total, pieces[k].astype(array.dtype))
            inside = jnp.where(passed, total, inside)
        before = combine(inside, before)
    return before


def in_one_piece(arrays, axis, dim, along):
    ends, at = ([], 0)
    for a in arrays[:-1]:
        at += a.shape[along]
        ends.append(at)
    both = jnp.concatenate(arrays, axis=along)
    return tuple(jnp.split(lax.all_gather(both, axis, axis=dim, tiled=True), ends, axis=along))


def split_up(array, dim, peers):
    shape = array.shape
    tiles = array.reshape(*shape[:dim], peers, shape[dim] // peers, *shape[dim + 1 :])
    return jnp.moveaxis(tiles, dim, 0)


def sum_at_owner(array, axis, dim):
    tiles = split_up(array, dim, lax.axis_size(axis))
    arrived = lax.all_to_all(tiles, axis, split_axis=0, concat_axis=0, tiled=True)
    return arrived.astype(jnp.float32).sum(axis=0)


def add_states(earlier, later):
    return earlier + later


def body(tokens, w_query, w_key, w_value, head_gain, w_out, norm_gain, w_gate, w_up, w_down):
    length = tokens.shape[0]
    width_here = tokens.shape[1]
    heads_here = w_query.shape[1] // HD
    features = lax.all_gather(tokens, "tp", axis=1, tiled=True)

    def project(weight):
        product = jnp.dot(features, weight, preferred_element_type=jnp.float32)
        return product.astype(jnp.bfloat16).reshape(length, heads_here, HD)

    query = project(w_query)
    keys_local = project(w_key)
    values_local = project(w_value)
    scores = jnp.einsum("ihd,jhd->hij", query, keys_local, preferred_element_type=jnp.float32)
    causal = jnp.arange(length)[:, None] >= jnp.arange(length)[None, :]
    scores = jnp.where(causal[None], scores, 0.0).astype(jnp.bfloat16)
    inside = jnp.einsum("hij,jhd->ihd", scores, values_local, preferred_element_type=jnp.float32)
    own_state = jnp.einsum(
        "jhd,jhe->hde", keys_local, values_local, preferred_element_type=jnp.float32
    )
    history = entering(own_state, SEQ, add_states, jnp.zeros_like(own_state))
    carried = jnp.einsum(
        "ihd,hde->ihe", query, history.astype(jnp.bfloat16), preferred_element_type=jnp.float32
    )
    mixed = inside + carried
    scale = lax.rsqrt(jnp.mean(mixed * mixed, axis=-1, keepdims=True) + 1e-06)
    normed = (mixed * scale * head_gain.reshape(heads_here, HD)).astype(jnp.bfloat16)
    normed = normed.reshape(length, heads_here * HD)
    partial_value = jnp.dot(normed, w_out, preferred_element_type=jnp.float32)
    own_column = lax.axis_index("tp") * width_here
    summed = lax.psum(partial_value.astype(jnp.bfloat16), "tp").astype(jnp.float32)
    resid_whole = features.astype(jnp.float32) + summed
    factor = lax.rsqrt(jnp.mean(resid_whole * resid_whole, axis=-1, keepdims=True) + 1e-05)
    ffn_in = (resid_whole * factor * norm_gain).astype(jnp.bfloat16)
    resid = lax.dynamic_slice_in_dim(resid_whole, own_column, width_here, 1)
    pieces = in_one_piece((w_gate, w_up), SEQ, 0, 1)
    gate_sum = jnp.dot(ffn_in, pieces[0], preferred_element_type=jnp.float32)
    upward_sum = jnp.dot(ffn_in, pieces[1], preferred_element_type=jnp.float32)
    hidden = (jax.nn.silu(gate_sum) * upward_sum).astype(jnp.bfloat16)
    terms = jnp.dot(
        hidden, lax.all_gather(w_down, SEQ, axis=1, tiled=True), preferred_element_type=jnp.float32
    )
    mlp_share = sum_at_owner(terms.astype(jnp.bfloat16), "tp", 1)
    return (resid + mlp_share).astype(jnp.bfloat16)


def solution(mesh):
    finer = Mesh(mesh.devices.reshape(4, 8, mesh.shape["tp"]), ("seq_0", "seq_1", "tp"))
    return jax.shard_map(
        body,
        mesh=finer,
        in_specs=(
            P(SEQ, "tp"),
            P(None, "tp"),
            P(None, "tp"),
            P(None, "tp"),
            P("tp"),
            P("tp", None),
            P(),
            P(SEQ, "tp"),
            P(SEQ, "tp"),
            P("tp", SEQ),
        ),
        out_specs=P(SEQ, "tp"),
        check_vma=False,
    )
```

profile of v0, /device:TPU:1, one launch (start us, length us, event | category | flops | bytes accessed | tf_op | source)
XLA Modules:
  0.0 356.1 jit_solution(3774338087254047791)
XLA Ops:
  7.4 0.0 copy-start
  7.4 0.0 all-gather.5.cloned.1.call-start
  7.4 0.7 all-gather.5.cloned.1.call-update
  8.1 0.0 all-reduce.2.cloned.1.call-start
  8.2 0.2 iota_compare_fusion
  8.3 39.5 %all-gather.5.cloned.1.call-done = bf16[768,2048]{1,0:T(8,128)(2,1)} async-done(((bf16[768,256]{1,0:T(8,128)(2,1)}), bf16[768,2048]{1,0:T(8,128)(2,1)}) %all-gather.5.cloned.1.call-update) | async-done | bytes 3145744 | tf_op jit(solution)/shard_map/all_gather | solution.py:59
  47.9 0.0 copy-start.1
  47.9 3.3 convolution_convert_fusion.2
  51.2 0.0 copy-done.1
  51.2 0.0 copy-start.5
  51.2 2.4 convolution_convert_fusion.4
  53.6 0.3 convolution_convert_fusion.5
  53.9 20.8 %all-gather = bf16[16,128,128]{2,1,0:T(8,128)(2,1)S(1)} all-gather(bf16[2,128,128]{2,1,0:T(8,128)(2,1)S(1)} %convolution_convert_fusion.5), channel_id=2, replica_groups=mesh['seq_0'=4,'seq_1'=8,'tp'=8] {'seq_1'}, dimensions={0}, use_global_device_ids=true | all-gather | bytes 589824 | tf_op jit(solution)/shard_map/all_gather | solution.py:20
  74.7 0.1 fusion.28
  74.7 9.7 %all_gather.22 = bf16[4,2,128,128]{3,2,1,0:T(8,128)(2,1)S(1)} all-gather(bf16[1,2,128,128]{3,2,1,0:T(8,128)(2,1)S(1)} %fusion.28), channel_id=1, replica_groups=mesh['seq_0'=4,'seq_1'=8,'tp'=8] {'seq_0'}, dimensions={0}, use_global_device_ids=true | all-gather | bytes 327680 | tf_op jit(solution)/shard_map/all_gather | solution.py:20
  84.5 0.0 copy-done.5
  84.5 1.1 convolution_convert_fusion.3
  85.6 0.0 copy-start.7
  85.6 0.7 copy-done.7
  86.3 1.3 fusion.29
  87.6 0.0 copy-start.4
  87.6 2.9 multiply_reduce_fusion.1
  90.5 0.0 copy-done.4
  90.5 0.1 multiply_convert_fusion.2
  90.6 0.0 copy-done
  90.6 2.7 convolution_convert_fusion.1
  93.4 0.0 copy-start.2
  93.4 0.0 all-reduce.2.cloned.1.call-update
  93.4 0.0 all-gather.7.cloned.1.call-start
  93.5 0.8 copy-done.2
  94.3 0.1 copy-done.3
  94.3 0.7 pad_maximum_fusion
  95.1 0.0 all-gather.7.cloned.1.call-update
  95.1 0.2 all-gather.9.cloned.1.call-start
  95.3 0.4 all-gather.9.cloned.1.call-update
  95.7 0.0 copy-start.6
  95.7 79.1 %all-reduce.2.cloned.1.call-done = bf16[768,2048]{1,0:T(8,128)(2,1)} async-done(((bf16[768,2048]{1,0:T(8,128)(2,1)}), bf16[768,2048]{1,0:T(8,128)(2,1)}) %all-reduce.2.cloned.1.call-update) | async-done | bytes 3145744 | tf_op jit(solution)/shard_map/psum | solution.py:85
  174.8 6.7 %convert_add_fusion = (f32[768,2048]{1,0:T(8,128)}, f32[768]{0:T(1024)S(1)}) fusion(bf16[768,2048]{1,0:T(8,128)(2,1)} %all-reduce.2.cloned.1.call-done, bf16[768,2048]{1,0:T(8,128)(2,1)} %all-gather.5.cloned.1.call-done), kind=kLoop, calls=%fused_computation.3 | loop fusion | flops 7863552 | bytes 12585984 | tf_op jit(solution)/shard_map/add | solution.py:86
  181.6 19.3 %all-gather.7.cloned.1.call-done = bf16[2048,2048]{1,0:T(8,128)(2,1)} async-done(((bf16[64,2048]{1,0:T(8,128)(2,1)}), bf16[2048,2048]{1,0:T(8,128)(2,1)}) %all-gather.7.cloned.1.call-update) | async-done | bytes 8388624 | tf_op jit(solution)/shard_map/all_gather | solution.py:36
  200.9 0.0 copy-done.6
  200.9 9.2 %fusion = f32[768,1024]{1,0:T(8,128)} fusion(bf16[2048,2048]{1,0:T(8,128)(2,1)} %all-gather.7.cloned.1.call-done, f32[2048]{0:T(1024)S(1)} %copy-done.6, f32[768]{0:T(1024)S(1)} %add_rsqrt_fusion.1, bf16[768,2048]{1,0:T(8,128)(2,1)} %all-reduce.2.cloned.1.call-done, bf16[768,2048]{1,0:T(8,128)(2,1)} %all-gather.5.cloned.1.call-done), kind=kOutput, calls=%fused_computation.5 | convolution fusion | flops 3230662656 | bytes 13642752 | tf_op jit(solution)/shard_map/dot_general | solution.py:92
  210.2 69.3 %all-gather.9.cloned.1.call-done = bf16[1024,2048]{0,1:T(8,128)(2,1)} async-done(((bf16[1024,64]{0,1:T(8,128)(2,1)}), bf16[1024,2048]{0,1:T(8,128)(2,1)}) %all-gather.9.cloned.1.call-update) | async-done | bytes 4194320 | tf_op jit(solution)/shard_map/all_gather | solution.py:95
  279.5 14.9 %convolution_convert_fusion = bf16[768,2048]{1,0:T(8,128)(2,1)} fusion(bf16[1024,2048]{0,1:T(8,128)(2,1)} %all-gather.9.cloned.1.call-done, f32[768,1024]{1,0:T(8,128)} %fusion, bf16[2048,2048]{1,0:T(8,128)(2,1)} %all-gather.7.cloned.1.call-done, f32[2048]{0:T(1024)S(1)} %copy-done.6, f32[768]{0:T(1024)S(1)} %add_rsqrt_fusion.1, ...), kind=kOutput, calls=%fused_computation.9 | convolution fusion | flops 6458179584 | bytes 20982784 | tf_op jit(solution)/shard_map/dot_general | solution.py:94
  294.4 3.7 %copy.23 = bf16[96,8,8,256]{3,2,0,1:T(8,128)(2,1)} copy(bf16[96,8,8,256]{3,2,1,0:T(8,128)(2,1)} %bitcast.58) | data formatting | bytes 6291456 | tf_op jit(solution)/shard_map/reshape | solution.py:41
  298.1 8.6 %all-to-all-start = ((bf16[8,768,256]{2,1,0:T(8,128)(2,1)}), bf16[8,768,256]{2,1,0:T(8,128)(2,1)}, u32[]{:S(2)}, u32[]{:S(2)}) async-start(bf16[8,768,256]{2,1,0:T(8,128)(2,1)} %bitcast.57), calls=%async_computation | async-start | bytes 6291456 | tf_op jit(solution)/shard_map/all_to_all | solution.py:47
  306.7 37.6 %all-to-all-done = bf16[8,768,256]{2,1,0:T(8,128)(2,1)} async-done(((bf16[8,768,256]{2,1,0:T(8,128)(2,1)}), bf16[8,768,256]{2,1,0:T(8,128)(2,1)}, u32[]{:S(2)}, u32[]{:S(2)}) %all-to-all-start) | async-done | bytes 3145760 | tf_op jit(solution)/shard_map/all_to_all | solution.py:47
  344.3 2.4 convert_reduce_fusion
  346.7 2.0 add_convert_fusion
  (3 shorter events, 0.0 us)
Async XLA Ops:
  7.4 83.3 %copy-start = (bf16[256,2048]{1,0:T(8,128)(2,1)S(1)}, bf16[256,2048]{1,0:T(8,128)(2,1)}, u32[]{:S(2)}) copy-start(bf16[256,2048]{1,0:T(8,128)(2,1)} %param.15) | copy-start | bytes 3145732
  7.4 40.5 %all-gather.5.cloned.1.call-start = ((), (), s32[]{:S(2)}) async-start(), calls=%async_computation.1 | async-start | bytes 3538944 | tf_op jit(solution)/shard_map/all_gather | solution.py:59
  8.1 166.7 %all-reduce.2.cloned.1.call-start = ((), (), s32[]{:S(2)}) async-start(), calls=%async_computation.2 | async-start | bytes 6291456 | tf_op jit(solution)/shard_map/psum | solution.py:85
  47.9 3.4 copy-start.1
  51.2 33.2 %copy-start.5 = (bf16[2048,256]{1,0:T(8,128)(2,1)S(1)}, bf16[2048,256]{1,0:T(8,128)(2,1)}, u32[]{:S(2)}) copy-start(bf16[2048,256]{1,0:T(8,128)(2,1)} %param.11) | copy-start | bytes 3145732
  85.6 0.7 copy-start.7
  87.6 2.9 copy-start.4
  93.4 0.9 copy-start.2
  93.4 1.0 copy-start.3
  93.4 107.5 %all-gather.7.cloned.1.call-start = ((), (), s32[]{:S(2)}) async-start(), calls=%async_computation.3 | async-start | bytes 8650752 | tf_op jit(solution)/shard_map/all_gather | solution.py:36
  95.1 184.4 %all-gather.9.cloned.1.call-start = ((), (), s32[]{:S(2)}) async-start(), calls=%async_computation.4 | async-start | bytes 4325376 | tf_op jit(solution)/shard_map/all_gather | solution.py:95
  95.7 105.2 %copy-start.6 = (f32[2048]{0:T(1024)S(1)}, f32[2048]{0:T(1024)}, u32[]{:S(2)}) copy-start(f32[2048]{0:T(1024)} %param.16) | copy-start | bytes 24580
  298.1 46.2 %all-to-all-start = ((bf16[8,768,256]{2,1,0:T(8,128)(2,1)}), bf16[8,768,256]{2,1,0:T(8,128)(2,1)}, u32[]{:S(2)}, u32[]{:S(2)}) async-start(bf16[8,768,256]{2,1,0:T(8,128)(2,1)} %bitcast.57), calls=%async_computation | async-start | bytes 6291456 | tf_op jit(solution)/shard_map/all_to_all | solution.py:47
Sparse Core Ops, SparseCore 0:
  10.0 37.8 all-gather.4
  93.5 81.2 all-reduce.1
Sparse Core Ops, SparseCore 1:
  96.5 104.4 all-gather.6
  203.4 76.1 all-gather.8
where the time goes:
time: 356 us
  waiting for transfers between devices  246 us (69%)
  matrix products  38.1 us (11%)
  blocking collectives  30.5 us (9%)
  between operations  15 us (4%)
  other arithmetic  12.2 us (3%)
  starting transfers between devices  8.92 us (3%)
  local copies, waits for them, and re-layouts  5.37 us (2%)
    psum x1, waiting for transfers between devices, body(): lax.psum(partial_value.astype(jnp.bfloat16), 'tp').astype(jnp.float32)  79.1 us
    all_gather x1, waiting for transfers between devices, body(): lax.all_gather(w_down, SEQ, axis=1, tiled=True)  69.3 us
    all_gather x1, waiting for transfers between devices, body(): features = lax.all_gather(tokens, 'tp', axis=1, tiled=True)  39.5 us
    all_to_all x1, waiting for transfers between devices, sum_at_owner(): lax.all_to_all(tiles, axis, split_axis=0, concat_axis=0, tiled=True)  37.6 us
    all_gather x2, blocking collectives, entering(): pieces = lax.all_gather(total.astype(jnp.bfloat16), axis)  30.5 us
    all_gather x1, waiting for transfers between devices, in_one_piece(): lax.all_gather(both, axis, axis=dim, tiled=True)  19.3 us
    dot_general x1, matrix products, body(): jnp.dot(hidden, lax.all_gather(w_down, SEQ, axis=1, tiled=True), preferre...  14.9 us
    dot_general x1, matrix products, body(): upward_sum = jnp.dot(ffn_in, pieces[1], preferred_element_type=jnp.float32)  9.24 us
  transfers between devices with their start and end apart: 5, of which 5 were waited for; matrix products, arithmetic and copies ran while one was open for 5% of the time, Pallas kernels for 0%

commit v1 on v0

--- a/solution.py
+++ b/solution.py
@@ -1,11 +1,21 @@
+import functools
 import jax
 import jax.numpy as jnp
 from jax import lax
 from jax.sharding import Mesh
 from jax.sharding import PartitionSpec as P
+from jax.lax import all_gather
 
 HD = 128
 SEQ = ("seq_0", "seq_1")
+
+
+def register_the_limits(array_here, row_axis):
+    row_out = jnp.concatenate(all_gather(array_here, axis_name=row_axis), axis=1)
+    return row_out
+
+
+order_task = functools.partial(register_the_limits, row_axis=SEQ)
 
 
 def nothing_yet(array, identity):
@@ -91,9 +101,7 @@
     gate_sum = jnp.dot(ffn_in, pieces[0], preferred_element_type=jnp.float32)
     upward_sum = jnp.dot(ffn_in, pieces[1], preferred_element_type=jnp.float32)
     hidden = (jax.nn.silu(gate_sum) * upward_sum).astype(jnp.bfloat16)
-    terms = jnp.dot(
-        hidden, lax.all_gather(w_down, SEQ, axis=1, tiled=True), preferred_element_type=jnp.float32
-    )
+    terms = jnp.dot(hidden, order_task(w_down), preferred_element_type=jnp.float32)
     mlp_share = sum_at_owner(terms.astype(jnp.bfloat16), "tp", 1)
     return (resid + mlp_share).astype(jnp.bfloat16)
 

time: 356 us -> 366 us (1.028)
  local copies, waits for them, and re-layouts: 5.37 us -> 13.5 us
  waiting for transfers between devices: 246 us -> 250 us
    all_gather x1, waiting for transfers between devices: 19.3 us -> 91 us  [in_one_piece(): lax.all_gather(both, axis, axis=dim, tiled=True)]
    all_gather x1, waiting for transfers between devices: 69.3 us -> 0.6 us  [register_the_limits(): all_gather(array_here, axis_name=row_axis)]
    reshape x0 -> x1, local copies, waits for them, and re-layouts: none -> 4.29 us  [register_the_limits(): jnp.concatenate(all_gather(array_here, axis_name=row_axis), axis=1)]
    unnamed x16 -> x17, local copies, waits for them, and re-layouts: 1.65 us -> 5.55 us
  transfers between devices with their start and end apart: 5 -> 5, of which waited for: 5 -> 5; matrix products, arithmetic and copies ran while one was open for 5% -> 4% of each run, Pallas kernels for 0% -> 0%
where the time goes in v1:
time: 366 us; the launch traced here: 365 us
  waiting for transfers between devices  250 us (68%)
  matrix products  38.3 us (10%)
  blocking collectives  30.5 us (8%)
  between operations  15 us (4%)
  local copies, waits for them, and re-layouts  13.5 us (4%)
  other arithmetic  12.1 us (3%)
  starting transfers between devices  6.1 us (2%)
    all_gather x1, waiting for transfers between devices, in_one_piece(): lax.all_gather(both, axis, axis=dim, tiled=True)  91 us
    psum x1, waiting for transfers between devices, body(): lax.psum(partial_value.astype(jnp.bfloat16), 'tp').astype(jnp.float32)  79.8 us
    all_gather x1, waiting for transfers between devices, body(): features = lax.all_gather(tokens, 'tp', axis=1, tiled=True)  39.5 us
    all_to_all x1, waiting for transfers between devices, sum_at_owner(): lax.all_to_all(tiles, axis, split_axis=0, concat_axis=0, tiled=True)  37.6 us
    all_gather x2, blocking collectives, entering(): pieces = lax.all_gather(total.astype(jnp.bfloat16), axis)  30.5 us
    dot_general x1, matrix products, body(): jnp.dot(hidden, order_task(w_down), preferred_element_type=jnp.float32)  15.1 us
    dot_general x1, matrix products, body(): upward_sum = jnp.dot(ffn_in, pieces[1], preferred_element_type=jnp.float32)  9.25 us
  transfers between devices with their start and end apart: 5, of which 5 were waited for; matrix products, arithmetic and copies ran while one was open for 4% of the time, Pallas kernels for 0%

profile of v1, /device:TPU:1, one launch (start us, length us, event | category | flops | bytes accessed | tf_op | source)
XLA Modules:
  0.0 365.2 jit_solution(699206692933125971)
XLA Ops:
  7.4 0.0 copy-start
  7.4 0.0 all-gather.6.cloned.1.call-start
  7.4 0.7 all-gather.6.cloned.1.call-update
  8.1 0.0 all-reduce.2.cloned.1.call-start
  8.2 0.2 iota_compare_fusion
  8.3 39.5 %all-gather.6.cloned.1.call-done = bf16[768,2048]{1,0:T(8,128)(2,1)} async-done(((bf16[768,256]{1,0:T(8,128)(2,1)}), bf16[768,2048]{1,0:T(8,128)(2,1)}) %all-gather.6.cloned.1.call-update) | async-done | bytes 3145744 | tf_op jit(solution)/shard_map/all_gather | solution.py:69
  47.9 0.0 copy-start.1
  47.9 3.3 convolution_convert_fusion.2
  51.2 0.0 copy-done.1
  51.2 0.0 copy-start.5
  51.2 2.4 convolution_convert_fusion.4
  53.6 0.3 convolution_convert_fusion.5
  53.9 20.8 %all-gather = bf16[16,128,128]{2,1,0:T(8,128)(2,1)S(1)} all-gather(bf16[2,128,128]{2,1,0:T(8,128)(2,1)S(1)} %convolution_convert_fusion.5), channel_id=2, replica_groups=mesh['seq_0'=4,'seq_1'=8,'tp'=8] {'seq_1'}, dimensions={0}, use_global_device_ids=true | all-gather | bytes 589824 | tf_op jit(solution)/shard_map/all_gather | solution.py:30
  74.7 0.1 fusion.28
  74.7 9.7 %all_gather.25 = bf16[4,2,128,128]{3,2,1,0:T(8,128)(2,1)S(1)} all-gather(bf16[1,2,128,128]{3,2,1,0:T(8,128)(2,1)S(1)} %fusion.28), channel_id=1, replica_groups=mesh['seq_0'=4,'seq_1'=8,'tp'=8] {'seq_0'}, dimensions={0}, use_global_device_ids=true | all-gather | bytes 327680 | tf_op jit(solution)/shard_map/all_gather | solution.py:30
  84.5 0.0 copy-done.5
  84.5 1.1 convolution_convert_fusion.3
  85.6 0.0 copy-start.7
  85.6 0.7 copy-done.7
  86.3 1.3 fusion.29
  87.6 2.9 multiply_reduce_fusion.1
  90.5 0.0 copy-done.4
  90.5 0.1 multiply_convert_fusion.2
  90.6 0.0 copy-done
  90.6 2.7 convolution_convert_fusion.1
  93.4 0.0 all-reduce.2.cloned.1.call-update
  93.4 0.0 all-gather.10.cloned.1.call-start
  93.5 0.5 all-gather.10.cloned.1.call-update
  94.0 0.2 all-gather.8.cloned.1.call-start
  94.2 0.1 copy-done.2
  94.3 0.1 copy-done.3
  94.3 0.7 pad_maximum_fusion
  95.1 0.0 all-gather.8.cloned.1.call-update
  95.1 79.8 %all-reduce.2.cloned.1.call-done = bf16[768,2048]{1,0:T(8,128)(2,1)} async-done(((bf16[768,2048]{1,0:T(8,128)(2,1)}), bf16[768,2048]{1,0:T(8,128)(2,1)}) %all-reduce.2.cloned.1.call-update) | async-done | bytes 3145744 | tf_op jit(solution)/shard_map/psum | solution.py:95
  174.9 6.6 %convert_add_fusion = (f32[768,2048]{1,0:T(8,128)}, f32[768]{0:T(1024)S(1)}) fusion(bf16[768,2048]{1,0:T(8,128)(2,1)} %all-reduce.2.cloned.1.call-done, bf16[768,2048]{1,0:T(8,128)(2,1)} %all-gather.6.cloned.1.call-done), kind=kLoop, calls=%fused_computation.3 | loop fusion | flops 7863552 | bytes 12585984 | tf_op jit(solution)/shard_map/add | solution.py:96
  181.4 0.6 all-gather.10.cloned.1.call-done
  182.0 4.6 %copy.36 = bf16[8,8,32,1024]{3,2,1,0:T(8,128)(2,1)S(1)} copy(bf16[8,8,32,1024]{3,1,2,0:T(8,128)(2,1)} %bitcast.66) | data formatting | bytes 8388608
  186.7 0.0 copy-start.6
  186.7 4.3 %copy.28 = bf16[1024,32,64]{0,2,1:T(8,128)(2,1)} copy(bf16[1024,32,64]{0,1,2:T(8,128)(2,1)S(1)} %bitcast.64) | data formatting | bytes 8388608 | tf_op jit(solution)/shard_map/reshape | solution.py:14
  191.0 91.0 %all-gather.8.cloned.1.call-done = bf16[2048,2048]{1,0:T(8,128)(2,1)} async-done(((bf16[64,2048]{1,0:T(8,128)(2,1)}), bf16[2048,2048]{1,0:T(8,128)(2,1)}) %all-gather.8.cloned.1.call-update) | async-done | bytes 8388624 | tf_op jit(solution)/shard_map/all_gather | solution.py:46
  281.9 0.0 copy-done.6
  281.9 9.2 %fusion = f32[768,1024]{1,0:T(8,128)} fusion(bf16[2048,2048]{1,0:T(8,128)(2,1)} %all-gather.8.cloned.1.call-done, f32[2048]{0:T(1024)S(1)} %copy-done.6, f32[768]{0:T(1024)S(1)} %add_rsqrt_fusion.1, bf16[768,2048]{1,0:T(8,128)(2,1)} %all-reduce.2.cloned.1.call-done, bf16[768,2048]{1,0:T(8,128)(2,1)} %all-gather.6.cloned.1.call-done), kind=kOutput, calls=%fused_computation.5 | convolution fusion | flops 3230662656 | bytes 13642752 | tf_op jit(solution)/shard_map/dot_general | solution.py:102
  291.2 15.1 %convolution_convert_fusion = bf16[768,2048]{1,0:T(8,128)(2,1)} fusion(bf16[1024,2048]{0,1:T(8,128)(2,1)} %bitcast.67, f32[768,1024]{1,0:T(8,128)} %fusion, bf16[2048,2048]{1,0:T(8,128)(2,1)} %all-gather.8.cloned.1.call-done, f32[2048]{0:T(1024)S(1)} %copy-done.6, f32[768]{0:T(1024)S(1)} %add_rsqrt_fusion.1, ...), kind=kOutput, calls=%fused_computation.9 | convolution fusion | flops 6458179584 | bytes 20982784 | tf_op jit(solution)/shard_map/dot_general | solution.py:104
  306.3 3.7 %copy.38 = bf16[96,8,8,256]{3,2,0,1:T(8,128)(2,1)} copy(bf16[96,8,8,256]{3,2,1,0:T(8,128)(2,1)} %bitcast.68) | data formatting | bytes 6291456 | tf_op jit(solution)/shard_map/reshape | solution.py:51
  310.0 5.8 %all-to-all-start = ((bf16[8,768,256]{2,1,0:T(8,128)(2,1)}), bf16[8,768,256]{2,1,0:T(8,128)(2,1)}, u32[]{:S(2)}, u32[]{:S(2)}) async-start(bf16[8,768,256]{2,1,0:T(8,128)(2,1)} %bitcast.65), calls=%async_computation | async-start | bytes 6291456 | tf_op jit(solution)/shard_map/all_to_all | solution.py:57
  315.8 37.6 %all-to-all-done = bf16[8,768,256]{2,1,0:T(8,128)(2,1)} async-done(((bf16[8,768,256]{2,1,0:T(8,128)(2,1)}), bf16[8,768,256]{2,1,0:T(8,128)(2,1)}, u32[]{:S(2)}, u32[]{:S(2)}) %all-to-all-start) | async-done | bytes 3145760 | tf_op jit(solution)/shard_map/all_to_all | solution.py:57
  353.3 2.4 convert_reduce_fusion
  355.7 2.0 add_convert_fusion
  (5 shorter events, 0.0 us)
Async XLA Ops:
  7.4 83.3 %copy-start = (bf16[256,2048]{1,0:T(8,128)(2,1)S(1)}, bf16[256,2048]{1,0:T(8,128)(2,1)}, u32[]{:S(2)}) copy-start(bf16[256,2048]{1,0:T(8,128)(2,1)} %param.15) | copy-start | bytes 3145732
  7.4 40.5 %all-gather.6.cloned.1.call-start = ((), (), s32[]{:S(2)}) async-start(), calls=%async_computation.1 | async-start | bytes 3538944 | tf_op jit(solution)/shard_map/all_gather | solution.py:69
  8.1 166.8 %all-reduce.2.cloned.1.call-start = ((), (), s32[]{:S(2)}) async-start(), calls=%async_computation.2 | async-start | bytes 6291456 | tf_op jit(solution)/shard_map/psum | solution.py:95
  47.9 3.4 copy-start.1
  51.2 33.2 %copy-start.5 = (bf16[2048,256]{1,0:T(8,128)(2,1)S(1)}, bf16[2048,256]{1,0:T(8,128)(2,1)}, u32[]{:S(2)}) copy-start(bf16[2048,256]{1,0:T(8,128)(2,1)} %param.11) | copy-start | bytes 3145732
  85.6 0.7 copy-start.7
  87.6 2.9 copy-start.4
  93.4 0.9 copy-start.2
  93.4 1.0 copy-start.3
  93.4 88.6 %all-gather.10.cloned.1.call-start = ((), (), s32[]{:S(2)}) async-start(), calls=%async_computation.4 | async-start | bytes 4325376 | tf_op jit(solution)/shard_map/all_gather | solution.py:14
  94.0 188.0 %all-gather.8.cloned.1.call-start = ((), (), s32[]{:S(2)}) async-start(), calls=%async_computation.3 | async-start | bytes 8650752 | tf_op jit(solution)/shard_map/all_gather | solution.py:46
  186.7 95.3 %copy-start.6 = (f32[2048]{0:T(1024)S(1)}, f32[2048]{0:T(1024)}, u32[]{:S(2)}) copy-start(f32[2048]{0:T(1024)} %param.16) | copy-start | bytes 24580
  310.0 43.4 %all-to-all-start = ((bf16[8,768,256]{2,1,0:T(8,128)(2,1)}), bf16[8,768,256]{2,1,0:T(8,128)(2,1)}, u32[]{:S(2)}, u32[]{:S(2)}) async-start(bf16[8,768,256]{2,1,0:T(8,128)(2,1)} %bitcast.65), calls=%async_computation | async-start | bytes 6291456 | tf_op jit(solution)/shard_map/all_to_all | solution.py:57
Sparse Core Ops, SparseCore 0:
  10.0 37.8 all-gather.5
  93.5 81.2 all-reduce.1
Sparse Core Ops, SparseCore 1:
  96.5 85.5 all-gather.9
  184.5 97.4 all-gather.7
